TPU v7x, 32 devices: a whole 2x2x4 slice. The times are simulated.
32 devices in a mesh: ka: 16 (over z, y, x), occ: 2 (over core).
Axes of the slice: x: 2, y: 2, z: 4, core: 2. Of those that a mesh axis runs over, the one named last changes fastest.
Arguments:
- factors: bfloat16 [32, 2, 192, 2, 768], P('ka'), may hold values from -0.23925781 to 0.23925781
- occupied_energy: float32 [2], replicated, may hold values from -2 to -0.5
- virtual_energy: bfloat16 [32, 192], P('ka'), may hold values from 0.5 to 3
- conserve: int32 [32, 2], P('ka'), may hold values from 0 to 31, as said below
- pair_lists: int32 [2, 4, 2], P(None, 'occ'), may hold values from 0 to 1, as said below
Outputs:
- density: float32 [32, 192, 2, 192], P('ka', 'occ')
Inputs may be any that keep to these rules, and one draw needn't show every extreme that they name: For a momentum ka among the 2 momenta of block d (momenta d * 2 to d * 2 + 1), (32 - conserve[ka, r]) mod 32 lies in block (d - r - 1) mod 16; the 2 momenta of one block name different momenta in each round. `pair_lists`: each entry is an ordered pair (i, j) of occupied orbitals; every round begins with the pairs (0, 0) and (1, 1); within a round no ordered pair repeats (4 of the 4 ordered pairs appear).
All inputs are finite; a program needn't handle non-finite values.
Results may differ from a plain program's by a relative error of at most 0.00082.
Values may be sent and summed in bfloat16 or wider, within the bound.
A program may use at most 128 MiB of HBM per device.

v0:
```python
import functools

import jax
import jax.numpy as jnp
from jax import lax
from jax.experimental import pallas as pl
from jax.experimental.pallas import tpu as pltpu
from jax.sharding import PartitionSpec as P

LANES = 128
BAND = 64
STEP = 16
PIECE = 8


def from_behind(array, axis, by):
    size = lax.axis_size(axis)
    return lax.ppermute(array, axis, [(i, (i + by) % size) for i in range(size)])


def build_mates(received, auxiliary):
    real_part = received[..., :auxiliary]
    imaginary = received[..., auxiliary:]
    turned = jnp.concatenate([-imaginary, real_part], axis=-1)
    return jnp.concatenate([received, turned], axis=-2)


def amplitude(left_rows, mate_rows, energy_left, energy_right, occupied_sum):
    values = lax.dot_general(
        left_rows, mate_rows, (((1,), (1,)), ((), ())), preferred_element_type=jnp.float32
    )
    denominator = energy_left[:, None] + energy_right[None, :] - occupied_sum
    return values / jnp.concatenate([denominator, denominator], axis=1)


def density_term(amplitudes, swapped):
    virtuals = amplitudes.shape[0]
    combined = (2.0 * amplitudes - swapped).astype(jnp.bfloat16)
    rounded = amplitudes.astype(jnp.bfloat16)
    turned = jnp.concatenate([-rounded[:, virtuals:], rounded[:, :virtuals]], axis=1)
    stacked = jnp.concatenate([rounded, turned], axis=0)
    return lax.dot_general(
        combined, stacked, (((1,), (1,)), ((), ())), preferred_element_type=jnp.float32
    )


def pair_term(own_block, mate_block, energy_left, energy_right, occupied_energy, pair_row):
    leading = pair_row[0]
    trailing = pair_row[1]
    occupied_sum = occupied_energy[leading] + occupied_energy[trailing]
    amplitudes = amplitude(
        own_block[leading], mate_block[trailing], energy_left, energy_right, occupied_sum
    )
    swapped = amplitude(
        own_block[trailing], mate_block[leading], energy_left, energy_right, occupied_sum
    )
    return density_term(amplitudes, swapped)


def general(factors, occupied_energy, virtual_energy, conserve, pair_lists):
    momenta = factors.shape[0]
    orbitals = factors.shape[1]
    virtuals = factors.shape[2]
    auxiliary = factors.shape[4]
    own = factors.reshape(momenta, orbitals, virtuals, 2 * auxiliary)
    energy_own = virtual_energy.astype(jnp.float32)
    density = jnp.zeros((momenta, virtuals, 2 * virtuals), jnp.float32)
    for round_index in range(conserve.shape[1]):
        portion = orbitals // lax.axis_size("occ")
        portion_block = lax.dynamic_slice_in_dim(
            factors, lax.axis_index("occ") * portion, portion, 1
        )
        shifted, energy_mate = from_behind((portion_block, virtual_energy), "ka", round_index + 1)
        received = lax.all_gather(shifted, "occ", axis=1, tiled=True)
        mates = build_mates(received.reshape(momenta, orbitals, virtuals, 2 * auxiliary), auxiliary)
        energy_mate = energy_mate.astype(jnp.float32)
        for local_index in range(momenta):
            chosen = (momenta - conserve[local_index, round_index] % momenta) % momenta
            mate_block = lax.dynamic_index_in_dim(mates, chosen, 0, keepdims=False)
            energy_right = lax.dynamic_index_in_dim(energy_mate, chosen, 0, keepdims=False)
            own_block = own[local_index]
            energy_left = energy_own[local_index]

            def add_pair(partial_sum, pair_row):
                term = pair_term(
                    own_block, mate_block, energy_left, energy_right, occupied_energy, pair_row
                )
                return (partial_sum + term, None)

            running, ignored = lax.scan(add_pair, density[local_index], pair_lists[round_index])
            density = density.at[local_index].set(running)
    shaped = density.reshape(momenta, virtuals, 2, virtuals)
    return lax.psum_scatter(shaped, "occ", scatter_dimension=1, tiled=True)


def fused_kernel(
    ring, virtuals, auxiliary,
    conserve_hbm, occupied_hbm, energy_hbm, factors_ref, out_ref,
    conserve_ref, occupied_ref, energy_ref, own_raw, mate_raw, own, mate, energy_in, energy_left, inverse, products, total, incoming, partial,
    small_sem, own_sem, far_send, far_recv, near_send, near_recv,
    energy_send, energy_recv, swap_send, swap_recv,
):
    mesh_id = pl.DeviceIdType.MESH
    me = lax.axis_index("ka")
    core = lax.axis_index("occ")
    other = 1 - core
    odd = lax.rem(me, 2)
    half = virtuals // 2
    pieces = virtuals // PIECE
    steps = virtuals // STEP
    bands = virtuals // BAND
    per_step = STEP // PIECE
    per_band = BAND // STEP

    def at(step):
        return lax.rem(me + step + ring, ring)

    near = at(1 - 2 * odd)

    def own_copy(momentum, index):
        return pltpu.make_async_copy(
            factors_ref.at[momentum], own_raw.at[momentum], own_sem.at[index]
        )

    def small_copies():
        return (
            pltpu.make_async_copy(conserve_hbm, conserve_ref, small_sem.at[0]),
            pltpu.make_async_copy(occupied_hbm, occupied_ref, small_sem.at[1]),
            pltpu.make_async_copy(energy_hbm, energy_ref, small_sem.at[2]),
        )

    barrier = pltpu.get_barrier_semaphore()
    for place in ((at(-2), core), (near, core), (me, other)):
        pl.semaphore_signal(barrier, inc=1, device_id=place, device_id_type=mesh_id)
    own_copy(core, 0).start()
    for copy in small_copies():
        copy.start()
    own_copy(other, 1).start()

    def piece_rows(piece):
        return pl.ds(pl.multiple_of(piece * PIECE, PIECE), PIECE)

    def step_rows(step):
        return pl.ds(pl.multiple_of(step * STEP, STEP), STEP)

    def far_copy(piece):
        return pltpu.make_async_remote_copy(
            src_ref=own_raw.at[core, :, piece_rows(piece)],
            dst_ref=mate_raw.at[1, :, piece_rows(piece)],
            send_sem=far_send.at[piece], recv_sem=far_recv.at[piece],
            device_id=(at(2), core), device_id_type=mesh_id,
        )

    def near_copy(piece, relay):
        source = mate_raw.at[1] if relay else own_raw.at[core]
        return pltpu.make_async_remote_copy(
            src_ref=source.at[:, piece_rows(piece)],
            dst_ref=mate_raw.at[0, :, piece_rows(piece)],
            send_sem=near_send.at[piece], recv_sem=near_recv.at[piece],
            device_id=(near, core), device_id_type=mesh_id,
        )

    def energy_far():
        return pltpu.make_async_remote_copy(
            src_ref=energy_ref, dst_ref=energy_in.at[1],
            send_sem=energy_send.at[1], recv_sem=energy_recv.at[1],
            device_id=(at(2), core), device_id_type=mesh_id,
        )

    def energy_near(relay):
        return pltpu.make_async_remote_copy(
            src_ref=energy_in.at[1] if relay else energy_ref, dst_ref=energy_in.at[0],
            send_sem=energy_send.at[0], recv_sem=energy_recv.at[0],
            device_id=(near, core), device_id_type=mesh_id,
        )

    own_copy(core, 0).wait()
    pl.semaphore_wait(barrier, 3)

    def send_piece(piece, carry):
        far_copy(piece).start()

        @pl.when(odd == 0)
        def _():
            near_copy(piece, False).start()

        return carry

    lax.fori_loop(0, 2, send_piece, 0)
    for copy in small_copies():
        copy.wait()
    energy_far().start()

    @pl.when(odd == 0)
    def _():
        energy_near(False).start()

    lax.fori_loop(2, pieces, send_piece, 0)

    chosen = []
    for slot in range(2):
        mirror = lax.rem(2 - lax.rem(conserve_ref[0, slot], 2), 2)
        chosen.append(jnp.where(mirror == core, 0, 1))

    own_copy(other, 1).wait()

    def forward(piece):
        far_copy(piece).wait_recv()

        @pl.when(odd == 1)
        def _():
            near_copy(piece, True).start()

    def shape_own(step, carry):
        for momentum in range(2):
            for orbital in range(2):
                row = pl.ds(pl.multiple_of(orbital * virtuals + step * STEP, STEP), STEP)
                for part in range(2):
                    own[momentum, row, pl.ds(part * auxiliary, auxiliary)] = own_raw[
                        momentum, orbital, step_rows(step), part, :
                    ]
        return carry

    def shape_mate(slot, step):
        band = step // per_band
        for orbital in range(2):
            real = mate_raw[slot, orbital, step_rows(step), 0, :]
            imaginary = mate_raw[slot, orbital, step_rows(step), 1, :]
            first = orbital * 2 * BAND + lax.rem(step, per_band) * STEP
            plain = pl.ds(pl.multiple_of(first, STEP), STEP)
            turned = pl.ds(pl.multiple_of(first + BAND, STEP), STEP)
            mate[slot, band, plain, pl.ds(0, auxiliary)] = real
            mate[slot, band, plain, pl.ds(auxiliary, auxiliary)] = imaginary
            mate[slot, band, turned, pl.ds(0, auxiliary)] = -imaginary
            mate[slot, band, turned, pl.ds(auxiliary, auxiliary)] = real

    def shape_energies():
        sums = [occupied_ref[0] + occupied_ref[0], occupied_ref[0] + occupied_ref[1]]
        sums.append(occupied_ref[1] + occupied_ref[1])
        diagonal = lax.broadcasted_iota(
            jnp.int32, (virtuals, virtuals), 0
        ) == lax.broadcasted_iota(jnp.int32, (virtuals, virtuals), 1)
        mine = energy_ref[...].astype(jnp.float32)
        for momentum in range(2):
            spread = jnp.where(diagonal, mine[momentum : momentum + 1, :], 0.0)
            column = jnp.sum(spread, axis=1, keepdims=True)
            energy_left[momentum] = jnp.broadcast_to(column, (virtuals, LANES))
        energy_near(False).wait_recv()
        for slot in range(2):
            theirs = energy_in[slot].astype(jnp.float32)
            theirs = jnp.where(core == 0, theirs[0:1, :], theirs[1:2, :])
            for band in range(bands):
                part = theirs[:, band * BAND : (band + 1) * BAND]
                row = jnp.concatenate([part, part], axis=1)
                base = energy_left[chosen[slot]] + row
                for kind in range(3):
                    inverse[slot, band, kind] = 1.0 / (base - sums[kind])

    sign = jnp.where(lax.broadcasted_iota(jnp.int32, (virtuals, LANES), 1) < BAND, -1.0, 1.0)

    def add_band(slot, band):
        momentum = jnp.where(slot == 1, chosen[1], chosen[0])
        products[...] = lax.dot_general(
            own[momentum], mate[slot, band], (((1,), (1,)), ((), ())),
            preferred_element_type=jnp.float32,
        )
        amplitudes = {}
        for i in range(2):
            for j in range(2):
                value = products[i * virtuals : (i + 1) * virtuals, j * LANES : (j + 1) * LANES]
                amplitudes[i, j] = value * inverse[slot, band, i + j]
        combined, rounded, turned = [], [], []
        for i in range(2):
            for j in range(2):
                this = amplitudes[i, j]
                combined.append((2.0 * this - amplitudes[j, i]).astype(jnp.bfloat16))
                rounded.append(this.astype(jnp.bfloat16))
                turned.append((pltpu.roll(this, BAND, 1) * sign).astype(jnp.bfloat16))
        left = jnp.concatenate(combined, axis=1)
        right = jnp.concatenate(
            [jnp.concatenate(rounded, axis=1), jnp.concatenate(turned, axis=1)], axis=0
        )
        total[slot] += lax.dot_general(
            left, right, (((1,), (1,)), ((), ())), preferred_element_type=jnp.float32
        )

    def far_step(step):
        for piece in range(per_step):
            forward(step * per_step + piece)
        shape_mate(1, step)

    def near_step(step):
        for piece in range(per_step):
            near_copy(step * per_step + piece, False).wait_recv()
        shape_mate(0, step)

    total[...] = jnp.zeros_like(total)
    lax.fori_loop(0, steps // 2, shape_own, 0)
    far_step(0)
    energy_far().wait_recv()

    @pl.when(odd == 1)
    def _():
        energy_near(True).start()

    lax.fori_loop(steps // 2, steps, shape_own, 0)
    far_step(1)
    shape_energies()

    def main_step(step, carry):
        @pl.when(step > 1)
        def _():
            far_step(step)

        near_step(step - 1)
        phase = lax.rem(step, per_band)
        ready = jnp.logical_and(step >= per_band, jnp.logical_or(phase == 1, phase == 2))

        @pl.when(ready)
        def _():
            add_band(2 - phase, step // per_band - 1)

        return carry

    lax.fori_loop(1, steps, main_step, 0)

    def swap_copy(slot):
        return pltpu.make_async_remote_copy(
            src_ref=total.at[slot, pl.ds(pl.multiple_of(other * half, half), half), :],
            dst_ref=incoming.at[slot],
            send_sem=swap_send.at[slot], recv_sem=swap_recv.at[slot],
            device_id=(me, other), device_id_type=mesh_id,
        )

    add_band(1, bands - 1)
    swap_copy(1).start()
    near_step(steps - 1)
    add_band(0, bands - 1)
    swap_copy(0).start()

    def drain(piece, carry):
        far_copy(piece).wait_send()
        near_copy(piece, False).wait_send()
        return carry

    lax.fori_loop(0, pieces, drain, 0)
    energy_far().wait_send()
    energy_near(False).wait_send()
    here = pl.ds(pl.multiple_of(core * half, half), half)
    swap_copy(1).wait()
    for momentum in range(2):
        known = jnp.where(chosen[1] == momentum, total[1, here, :], incoming[1])
        partial[momentum] = known + jnp.where(chosen[0] == momentum, total[0, here, :], 0.0)
    swap_copy(0).wait()
    for momentum in range(2):
        value = partial[momentum] + jnp.where(chosen[0] == momentum, 0.0, incoming[0])
        for part in range(2):
            out_ref[momentum, :, part, :] = value[:, part * virtuals : (part + 1) * virtuals]


def fused(factors, occupied_energy, virtual_energy, conserve, pair_lists):
    momenta, orbitals, virtuals, parts, auxiliary = factors.shape
    ring = lax.axis_size("ka")
    pieces = virtuals // PIECE
    bands = virtuals // BAND
    dma = pltpu.SemaphoreType.DMA
    return pl.pallas_call(
        functools.partial(fused_kernel, ring, virtuals, auxiliary),
        out_shape=pltpu.VMEM((momenta, virtuals // 2, 2, virtuals), jnp.float32),
        in_specs=[
            pl.BlockSpec(memory_space=pltpu.HBM),
            pl.BlockSpec(memory_space=pltpu.HBM),
            pl.BlockSpec(memory_space=pltpu.HBM),
            pl.BlockSpec(memory_space=pltpu.HBM),
        ],
        out_specs=pl.BlockSpec(memory_space=pltpu.VMEM),
        scratch_shapes=[
            pltpu.SMEM(conserve.shape, conserve.dtype),
            pltpu.SMEM(occupied_energy.shape, occupied_energy.dtype),
            pltpu.VMEM(virtual_energy.shape, virtual_energy.dtype),
            pltpu.VMEM((momenta, orbitals, virtuals, parts, auxiliary), jnp.bfloat16),
            pltpu.VMEM((2, orbitals, virtuals, parts, auxiliary), jnp.bfloat16),
            pltpu.VMEM((momenta, orbitals * virtuals, parts * auxiliary), jnp.bfloat16),
            pltpu.VMEM((2, bands, orbitals * 2 * BAND, parts * auxiliary), jnp.bfloat16),
            pltpu.VMEM((2, momenta, virtuals), jnp.bfloat16),
            pltpu.VMEM((momenta, virtuals, LANES), jnp.float32),
            pltpu.VMEM((2, bands, 3, virtuals, LANES), jnp.float32),
            pltpu.VMEM((orbitals * virtuals, orbitals * 2 * BAND), jnp.float32),
            pltpu.VMEM((2, virtuals, 2 * virtuals), jnp.float32),
            pltpu.VMEM((2, virtuals // 2, 2 * virtuals), jnp.float32),
            pltpu.VMEM((2, virtuals // 2, 2 * virtuals), jnp.float32),
            dma((3,)), dma((2,)),
            dma((pieces,)), dma((pieces,)), dma((pieces,)), dma((pieces,)),
            dma((2,)), dma((2,)), dma((2,)), dma((2,)),
        ],
        compiler_params=pltpu.CompilerParams(
            collective_id=0, has_side_effects=True, vmem_limit_bytes=54 * 1024 * 1024
        ),
        name="density",
    )(conserve, occupied_energy, virtual_energy, factors)


def local(factors, occupied_energy, virtual_energy, conserve, pair_lists):
    momenta, orbitals, virtuals, parts, auxiliary = factors.shape
    rounds, pairs = pair_lists.shape[:2]
    ring, holders = lax.axis_size("ka"), lax.axis_size("occ")
    whole_square = pairs * holders == orbitals * orbitals
    fits = momenta == 2 and orbitals == 2 and holders == 2 and rounds == 2
    even = ring % 2 == 0 and ring > 4 and virtuals % BAND == 0 and auxiliary % LANES == 0
    chosen = fused if whole_square and fits and even else general
    return chosen(factors, occupied_energy, virtual_energy, conserve, pair_lists)


def solution(mesh):
    in_specs = (
        P("ka", None, None, None, None),
        P(),
        P("ka", None),
        P("ka", None),
        P(None, "occ", None),
    )
    out_specs = P("ka", "occ", None, None)
    return jax.shard_map(local, mesh=mesh, in_specs=in_specs, out_specs=out_specs, check_vma=False)
```

profile of v0, /device:TPU:0, one launch (start us, length us, event | category | flops | bytes accessed | tf_op | source)
XLA Modules:
  0.0 42.3 jit_solution(16124680420717331305)
XLA Ops:
  0.0 41.6 %density.1 = f32[2,96,2,192]{3,2,1,0:T(2,128)S(1)} custom-call(s32[2,2]{1,0:T(2,128)} %conserve_hbm.1, f32[2]{0:T(128)} %occupied_hbm.1, bf16[2,192]{1,0:T(2,128)(2,1)} %energy_hbm.1, bf16[2,2,192,2,768]{4,3,2,1,0:T(2,128)(2,1)} %factors_ref.1), custom_call_target="tpu_custom_call" | custom-call | tf_op jit(solution)/shard_map/density/pallas_call | solution.py:367
  41.6 0.7 %copy.6 = f32[2,96,2,192]{3,2,1,0:T(2,128)} copy(f32[2,96,2,192]{3,2,1,0:T(2,128)S(1)} %density.1) | data formatting | bytes 589824
where the time goes:
time: 42.5 us; the launch traced here: 42.3 us
  Pallas kernels  41.6 us (98%)
  local copies, waits for them, and re-layouts  0.75 us (2%)
    pallas_call x1, Pallas kernels, fused(): pl.pallas_call(functools.partial(fused_kernel, ring, virtuals, auxiliary)...  41.6 us

commit v1 on v0

--- a/solution.py
+++ b/solution.py
@@ -96,7 +96,7 @@
 def fused_kernel(
     ring, virtuals, auxiliary,
     conserve_hbm, occupied_hbm, energy_hbm, factors_ref, out_ref,
-    conserve_ref, occupied_ref, energy_ref, own_raw, mate_raw, own, mate, energy_in, energy_left, inverse, products, total, incoming, partial,
+    conserve_ref, occupied_ref, energy_ref, own_raw, mate_raw, own, mate, energy_in, energy_left, inverse, products, total, outgoing, incoming,
     small_sem, own_sem, far_send, far_recv, near_send, near_recv,
     energy_send, energy_recv, swap_send, swap_recv,
 ):
@@ -111,6 +111,8 @@
     bands = virtuals // BAND
     per_step = STEP // PIECE
     per_band = BAND // STEP
+    tiles = pl.cdiv(virtuals, LANES)
+    stride = 2 * tiles
 
     def at(step):
         return lax.rem(me + step + ring, ring)
@@ -277,17 +279,12 @@
                 rounded.append(this.astype(jnp.bfloat16))
                 turned.append((pltpu.roll(this, BAND, 1) * sign).astype(jnp.bfloat16))
         left = jnp.concatenate(combined, axis=1)
-        right = jnp.concatenate(
-            [jnp.concatenate(rounded, axis=1), jnp.concatenate(turned, axis=1)], axis=0
-        )
-        total[slot] += lax.dot_general(
-            left, right, (((1,), (1,)), ((), ())), preferred_element_type=jnp.float32
-        )
-
-    def far_step(step):
-        for piece in range(per_step):
-            forward(step * per_step + piece)
-        shape_mate(1, step)
+        spare = jnp.zeros((tiles * LANES - virtuals, left.shape[1]), jnp.bfloat16)
+        for part, pieces_of in enumerate((rounded, turned)):
+            right = jnp.concatenate([jnp.concatenate(pieces_of, axis=1), spare], axis=0)
+            total[slot, part] += lax.dot_general(
+                left, right, (((1,), (1,)), ((), ())), preferred_element_type=jnp.float32
+            )
 
     def near_step(step):
         for piece in range(per_step):
@@ -295,48 +292,79 @@
         shape_mate(0, step)
 
     total[...] = jnp.zeros_like(total)
-    lax.fori_loop(0, steps // 2, shape_own, 0)
-    far_step(0)
-    energy_far().wait_recv()
-
-    @pl.when(odd == 1)
-    def _():
-        energy_near(True).start()
-
-    lax.fori_loop(steps // 2, steps, shape_own, 0)
-    far_step(1)
-    shape_energies()
-
-    def main_step(step, carry):
-        @pl.when(step > 1)
-        def _():
-            far_step(step)
-
-        near_step(step - 1)
-        phase = lax.rem(step, per_band)
-        ready = jnp.logical_and(step >= per_band, jnp.logical_or(phase == 1, phase == 2))
+    early = steps - (BAND // PIECE - 1)
+    lax.fori_loop(0, early, shape_own, 0)
+
+    def main_step(piece, carry):
+        forward(piece)
+
+        @pl.when(piece == 1)
+        def _():
+            energy_far().wait_recv()
+
+            @pl.when(odd == 1)
+            def _():
+                energy_near(True).start()
+
+        even_piece = lax.rem(piece, 2) == 0
+
+        @pl.when(lax.rem(piece, per_step) == per_step - 1)
+        def _():
+            shape_mate(1, piece // per_step)
+
+        @pl.when(jnp.logical_and(even_piece, piece >= 4))
+        def _():
+            near_step(piece // 2 - 2)
+
+        @pl.when(piece < steps - early)
+        def _():
+            shape_own(early + piece, 0)
+
+        @pl.when(piece == steps - early)
+        def _():
+            shape_energies()
+
+        phase = lax.rem(piece, BAND // PIECE)
+        ready = jnp.logical_and(piece >= BAND // PIECE, jnp.logical_or(phase == 0, phase == 3))
 
         @pl.when(ready)
         def _():
-            add_band(2 - phase, step // per_band - 1)
+            add_band(jnp.where(phase == 0, 1, 0), piece // (BAND // PIECE) - 1)
 
         return carry
 
-    lax.fori_loop(1, steps, main_step, 0)
+    lax.fori_loop(0, pieces, main_step, 0)
 
     def swap_copy(slot):
         return pltpu.make_async_remote_copy(
-            src_ref=total.at[slot, pl.ds(pl.multiple_of(other * half, half), half), :],
-            dst_ref=incoming.at[slot],
+            src_ref=outgoing.at[slot], dst_ref=incoming.at[slot],
             send_sem=swap_send.at[slot], recv_sem=swap_recv.at[slot],
             device_id=(me, other), device_id_type=mesh_id,
         )
 
+    def half_rows(which):
+        return pl.ds(pl.multiple_of(which * half, half), half)
+
+    def places():
+        for part in range(2):
+            for tile in range(tiles):
+                yield part, pl.ds(tile * LANES, LANES), pl.ds(tile * 2 + part, half, stride)
+
+    def swap_start(slot):
+        for part, lanes, spots in places():
+            outgoing[slot, spots, :] = total[slot, part, half_rows(other), lanes]
+        swap_copy(slot).start()
+
+    near_step(steps - 2)
     add_band(1, bands - 1)
-    swap_copy(1).start()
+    swap_start(1)
+    for momentum in range(2):
+        for part, lanes, spots in places():
+            known = total[1, part, half_rows(core), lanes]
+            out_ref[momentum, spots, :] = jnp.where(chosen[1] == momentum, known, 0.0)
     near_step(steps - 1)
     add_band(0, bands - 1)
-    swap_copy(0).start()
+    swap_start(0)
 
     def drain(piece, carry):
         far_copy(piece).wait_send()
@@ -346,16 +374,15 @@
     lax.fori_loop(0, pieces, drain, 0)
     energy_far().wait_send()
     energy_near(False).wait_send()
-    here = pl.ds(pl.multiple_of(core * half, half), half)
     swap_copy(1).wait()
     for momentum in range(2):
-        known = jnp.where(chosen[1] == momentum, total[1, here, :], incoming[1])
-        partial[momentum] = known + jnp.where(chosen[0] == momentum, total[0, here, :], 0.0)
+        out_ref[momentum] += jnp.where(chosen[1] == momentum, 0.0, incoming[1])
+        for part, lanes, spots in places():
+            known = total[0, part, half_rows(core), lanes]
+            out_ref[momentum, spots, :] += jnp.where(chosen[0] == momentum, known, 0.0)
     swap_copy(0).wait()
     for momentum in range(2):
-        value = partial[momentum] + jnp.where(chosen[0] == momentum, 0.0, incoming[0])
-        for part in range(2):
-            out_ref[momentum, :, part, :] = value[:, part * virtuals : (part + 1) * virtuals]
+        out_ref[momentum] += jnp.where(chosen[0] == momentum, 0.0, incoming[0])
 
 
 def fused(factors, occupied_energy, virtual_energy, conserve, pair_lists):
@@ -363,10 +390,13 @@
     ring = lax.axis_size("ka")
     pieces = virtuals // PIECE
     bands = virtuals // BAND
+    half = virtuals // 2
+    tiles = pl.cdiv(virtuals, LANES)
+    packed = (half * 2 * tiles, LANES)
     dma = pltpu.SemaphoreType.DMA
-    return pl.pallas_call(
+    density = pl.pallas_call(
         functools.partial(fused_kernel, ring, virtuals, auxiliary),
-        out_shape=pltpu.VMEM((momenta, virtuals // 2, 2, virtuals), jnp.float32),
+        out_shape=pltpu.VMEM((momenta, *packed), jnp.float32),
         in_specs=[
             pl.BlockSpec(memory_space=pltpu.HBM),
             pl.BlockSpec(memory_space=pltpu.HBM),
@@ -386,9 +416,9 @@
             pltpu.VMEM((momenta, virtuals, LANES), jnp.float32),
             pltpu.VMEM((2, bands, 3, virtuals, LANES), jnp.float32),
             pltpu.VMEM((orbitals * virtuals, orbitals * 2 * BAND), jnp.float32),
-            pltpu.VMEM((2, virtuals, 2 * virtuals), jnp.float32),
-            pltpu.VMEM((2, virtuals // 2, 2 * virtuals), jnp.float32),
-            pltpu.VMEM((2, virtuals // 2, 2 * virtuals), jnp.float32),
+            pltpu.VMEM((2, 2, virtuals, tiles * LANES), jnp.float32),
+            pltpu.VMEM((2, *packed), jnp.float32),
+            pltpu.VMEM((2, *packed), jnp.float32),
             dma((3,)), dma((2,)),
             dma((pieces,)), dma((pieces,)), dma((pieces,)), dma((pieces,)),
             dma((2,)), dma((2,)), dma((2,)), dma((2,)),
@@ -398,6 +428,8 @@
         ),
         name="density",
     )(conserve, occupied_energy, virtual_energy, factors)
+    split = density.reshape(momenta, half, tiles, 2, LANES).transpose(0, 1, 3, 2, 4)
+    return split.reshape(momenta, half, 2, tiles * LANES)[..., :virtuals]
 
 
 def local(factors, occupied_energy, virtual_energy, conserve, pair_lists):
@@ -406,8 +438,9 @@
     ring, holders = lax.axis_size("ka"), lax.axis_size("occ")
     whole_square = pairs * holders == orbitals * orbitals
     fits = momenta == 2 and orbitals == 2 and holders == 2 and rounds == 2
-    even = ring % 2 == 0 and ring > 4 and virtuals % BAND == 0 and auxiliary % LANES == 0
-    chosen = fused if whole_square and fits and even else general
+    even = ring % 2 == 0 and ring > 4 and auxiliary % LANES == 0
+    banded = virtuals % BAND == 0 and virtuals >= 2 * BAND
+    chosen = fused if whole_square and fits and even and banded else general
     return chosen(factors, occupied_energy, virtual_energy, conserve, pair_lists)
 
 

time: 42.5 us -> 41.7 us (0.981)
  Pallas kernels: 41.6 us -> 40.8 us
    pallas_call x1, Pallas kernels: 41.6 us -> 40.8 us  [fused(): pl.pallas_call(functools.partial(fused_kernel, ring, virtuals, auxiliary)...]
where the time goes in v1:
time: 41.7 us; the launch traced here: 41.6 us
  Pallas kernels  40.8 us (98%)
  local copies, waits for them, and re-layouts  0.75 us (2%)
    pallas_call x1, Pallas kernels, fused(): pl.pallas_call(functools.partial(fused_kernel, ring, virtuals, auxiliary)...  40.8 us

profile of v1, /device:TPU:0, one launch (start us, length us, event | category | flops | bytes accessed | tf_op | source)
XLA Modules:
  0.0 41.6 jit_solution(15138750748082702943)
XLA Ops:
  0.0 40.8 %density.1 = f32[2,384,128]{2,1,0:T(8,128)S(1)} custom-call(s32[2,2]{1,0:T(2,128)} %conserve_hbm.1, f32[2]{0:T(128)} %occupied_hbm.1, bf16[2,192]{1,0:T(2,128)(2,1)} %energy_hbm.1, bf16[2,2,192,2,768]{4,3,2,1,0:T(2,128)(2,1)} %factors_ref.1), custom_call_target="tpu_custom_call" | custom-call | tf_op jit(solution)/shard_map/density/pallas_call | solution.py:397
  40.8 0.7 %copy.7 = f32[2,96,2,192]{3,2,1,0:T(2,128)} copy(f32[2,96,2,192]{3,2,1,0:T(2,128)S(1)} %bitcast.6) | data formatting | bytes 589824

commit v2 on v1

--- a/solution.py
+++ b/solution.py
@@ -11,6 +11,7 @@
 BAND = 64
 STEP = 16
 PIECE = 8
+LAST = 3
 
 
 def from_behind(array, axis, by):
@@ -96,9 +97,9 @@
 def fused_kernel(
     ring, virtuals, auxiliary,
     conserve_hbm, occupied_hbm, energy_hbm, factors_ref, out_ref,
-    conserve_ref, occupied_ref, energy_ref, own_raw, mate_raw, own, mate, energy_in, energy_left, inverse, products, total, outgoing, incoming,
+    conserve_ref, occupied_ref, energy_ref, own_raw, mate_raw, side, own, mate, energy_in, energy_left, inverse, products, total, outgoing, incoming,
     small_sem, own_sem, far_send, far_recv, near_send, near_recv,
-    energy_send, energy_recv, swap_send, swap_recv,
+    energy_send, energy_recv, swap_send, swap_recv, side_send, side_recv,
 ):
     mesh_id = pl.DeviceIdType.MESH
     me = lax.axis_index("ka")
@@ -134,6 +135,13 @@
     barrier = pltpu.get_barrier_semaphore()
     for place in ((at(-2), core), (near, core), (me, other)):
         pl.semaphore_signal(barrier, inc=1, device_id=place, device_id_type=mesh_id)
+    for listener, speaker in ((0, ring - 4), (ring - 4, ring - 1)):
+        @pl.when(me == listener)
+        def _():
+            pl.semaphore_signal(
+                barrier, inc=1, device_id=(speaker, core), device_id_type=mesh_id
+            )
+
     own_copy(core, 0).start()
     for copy in small_copies():
         copy.start()
@@ -147,19 +155,39 @@
 
     def far_copy(piece):
         return pltpu.make_async_remote_copy(
-            src_ref=own_raw.at[core, :, piece_rows(piece)],
+            src_ref=factors_ref.at[core, :, piece_rows(piece)],
             dst_ref=mate_raw.at[1, :, piece_rows(piece)],
-            send_sem=far_send.at[piece], recv_sem=far_recv.at[piece],
+            send_sem=far_send.at[0], recv_sem=far_recv.at[piece],
             device_id=(at(2), core), device_id_type=mesh_id,
         )
 
     def near_copy(piece, relay):
-        source = mate_raw.at[1] if relay else own_raw.at[core]
+        source = mate_raw.at[1] if relay else factors_ref.at[core]
         return pltpu.make_async_remote_copy(
             src_ref=source.at[:, piece_rows(piece)],
             dst_ref=mate_raw.at[0, :, piece_rows(piece)],
-            send_sem=near_send.at[piece], recv_sem=near_recv.at[piece],
+            send_sem=near_send.at[0], recv_sem=near_recv.at[piece // per_step],
             device_id=(near, core), device_id_type=mesh_id,
+        )
+
+    def near_arrival(step):
+        rows = mate_raw.at[0, :, step_rows(step)]
+        return pltpu.make_async_copy(rows, rows, near_recv.at[step])
+
+    def lend_copy(slot):
+        piece = pieces - LAST + slot
+        return pltpu.make_async_remote_copy(
+            src_ref=factors_ref.at[core, :, piece_rows(piece)], dst_ref=side.at[slot],
+            send_sem=side_send.at[0], recv_sem=side_recv.at[slot],
+            device_id=(ring - 4, core), device_id_type=mesh_id,
+        )
+
+    def carry_copy(slot):
+        piece = pieces - LAST + slot
+        return pltpu.make_async_remote_copy(
+            src_ref=side.at[slot], dst_ref=mate_raw.at[0, :, piece_rows(piece)],
+            send_sem=side_send.at[0], recv_sem=near_recv.at[piece // per_step],
+            device_id=(0, core), device_id_type=mesh_id,
         )
 
     def energy_far():
@@ -176,8 +204,13 @@
             device_id=(near, core), device_id_type=mesh_id,
         )
 
-    own_copy(core, 0).wait()
-    pl.semaphore_wait(barrier, 3)
+    greeters = jnp.where(jnp.logical_or(me == ring - 1, me == ring - 4), 4, 3)
+    pl.semaphore_wait(barrier, greeters)
+
+    @pl.when(me == ring - 1)
+    def _():
+        for slot in range(LAST):
+            lend_copy(slot).start()
 
     def send_piece(piece, carry):
         far_copy(piece).start()
@@ -204,12 +237,13 @@
         mirror = lax.rem(2 - lax.rem(conserve_ref[0, slot], 2), 2)
         chosen.append(jnp.where(mirror == core, 0, 1))
 
+    own_copy(core, 0).wait()
     own_copy(other, 1).wait()
 
     def forward(piece):
         far_copy(piece).wait_recv()
 
-        @pl.when(odd == 1)
+        @pl.when(jnp.logical_and(odd == 1, jnp.logical_or(me != 1, piece < pieces - LAST)))
         def _():
             near_copy(piece, True).start()
 
@@ -287,8 +321,7 @@
             )
 
     def near_step(step):
-        for piece in range(per_step):
-            near_copy(step * per_step + piece, False).wait_recv()
+        near_arrival(step).wait()
         shape_mate(0, step)
 
     total[...] = jnp.zeros_like(total)
@@ -298,6 +331,16 @@
     def main_step(piece, carry):
         forward(piece)
 
+        for slot in range(LAST):
+            @pl.when(jnp.logical_and(me == ring - 4, piece == slot + 8))
+            def _():
+                lend_copy(slot).wait_recv()
+                carry_copy(slot).start()
+
+        @pl.when(jnp.logical_and(me == 0, piece == pieces - 3))
+        def _():
+            near_step(steps - 1)
+
         @pl.when(piece == 1)
         def _():
             energy_far().wait_recv()
@@ -333,7 +376,7 @@
 
         return carry
 
-    lax.fori_loop(0, pieces, main_step, 0)
+    lax.fori_loop(0, pieces - per_step, main_step, 0)
 
     def swap_copy(slot):
         return pltpu.make_async_remote_copy(
@@ -355,34 +398,75 @@
             outgoing[slot, spots, :] = total[slot, part, half_rows(other), lanes]
         swap_copy(slot).start()
 
-    near_step(steps - 2)
-    add_band(1, bands - 1)
-    swap_start(1)
-    for momentum in range(2):
-        for part, lanes, spots in places():
-            known = total[1, part, half_rows(core), lanes]
-            out_ref[momentum, spots, :] = jnp.where(chosen[1] == momentum, known, 0.0)
-    near_step(steps - 1)
-    add_band(0, bands - 1)
-    swap_start(0)
-
-    def drain(piece, carry):
-        far_copy(piece).wait_send()
-        near_copy(piece, False).wait_send()
-        return carry
-
-    lax.fori_loop(0, pieces, drain, 0)
+    def sent(done, semaphore):
+        pltpu.make_async_copy(done, done, semaphore).wait()
+
+    def finish(first, second, before_first, before_second):
+        before_first()
+        add_band(first, bands - 1)
+        swap_start(first)
+        for momentum in range(2):
+            for part, lanes, spots in places():
+                known = total[first, part, half_rows(core), lanes]
+                out_ref[momentum, spots, :] = jnp.where(chosen[first] == momentum, known, 0.0)
+        before_second()
+        add_band(second, bands - 1)
+        swap_start(second)
+        swap_copy(first).wait()
+        for momentum in range(2):
+            out_ref[momentum] += jnp.where(chosen[first] == momentum, 0.0, incoming[first])
+            for part, lanes, spots in places():
+                known = total[second, part, half_rows(core), lanes]
+                out_ref[momentum, spots, :] += jnp.where(chosen[second] == momentum, known, 0.0)
+        sent(own_raw.at[core], far_send.at[0])
+        swap_copy(second).wait()
+        for momentum in range(2):
+            out_ref[momentum] += jnp.where(chosen[second] == momentum, 0.0, incoming[second])
+
+    near_first = jnp.logical_or(me == 0, me == ring - 4)
+
+    @pl.when(near_first)
+    def _():
+        def near_rest():
+            near_step(steps - 3)
+            near_step(steps - 2)
+
+            @pl.when(me != 0)
+            def _():
+                near_step(steps - 1)
+
+        def far_rest():
+            for piece in range(pieces - per_step, pieces):
+                forward(piece)
+            shape_mate(1, steps - 1)
+
+        finish(0, 1, near_rest, far_rest)
+
+    @pl.when(jnp.logical_not(near_first))
+    def _():
+        def far_rest():
+            forward(pieces - 2)
+            near_step(steps - 3)
+            forward(pieces - 1)
+            shape_mate(1, steps - 1)
+            near_step(steps - 2)
+
+        finish(1, 0, far_rest, lambda: near_step(steps - 1))
+
     energy_far().wait_send()
     energy_near(False).wait_send()
-    swap_copy(1).wait()
-    for momentum in range(2):
-        out_ref[momentum] += jnp.where(chosen[1] == momentum, 0.0, incoming[1])
-        for part, lanes, spots in places():
-            known = total[0, part, half_rows(core), lanes]
-            out_ref[momentum, spots, :] += jnp.where(chosen[0] == momentum, known, 0.0)
-    swap_copy(0).wait()
-    for momentum in range(2):
-        out_ref[momentum] += jnp.where(chosen[0] == momentum, 0.0, incoming[0])
+
+    @pl.when(me == 1)
+    def _():
+        sent(own_raw.at[core, :, pl.ds(0, virtuals - LAST * PIECE)], near_send.at[0])
+
+    @pl.when(me != 1)
+    def _():
+        sent(own_raw.at[core], near_send.at[0])
+
+    @pl.when(jnp.logical_or(me == ring - 1, me == ring - 4))
+    def _():
+        sent(side, side_send.at[0])
 
 
 def fused(factors, occupied_energy, virtual_energy, conserve, pair_lists):
@@ -410,6 +494,7 @@
             pltpu.VMEM(virtual_energy.shape, virtual_energy.dtype),
             pltpu.VMEM((momenta, orbitals, virtuals, parts, auxiliary), jnp.bfloat16),
             pltpu.VMEM((2, orbitals, virtuals, parts, auxiliary), jnp.bfloat16),
+            pltpu.VMEM((LAST, orbitals, PIECE, parts, auxiliary), jnp.bfloat16),
             pltpu.VMEM((momenta, orbitals * virtuals, parts * auxiliary), jnp.bfloat16),
             pltpu.VMEM((2, bands, orbitals * 2 * BAND, parts * auxiliary), jnp.bfloat16),
             pltpu.VMEM((2, momenta, virtuals), jnp.bfloat16),
@@ -420,8 +505,9 @@
             pltpu.VMEM((2, *packed), jnp.float32),
             pltpu.VMEM((2, *packed), jnp.float32),
             dma((3,)), dma((2,)),
-            dma((pieces,)), dma((pieces,)), dma((pieces,)), dma((pieces,)),
+            dma((1,)), dma((pieces,)), dma((1,)), dma((virtuals // STEP,)),
             dma((2,)), dma((2,)), dma((2,)), dma((2,)),
+            dma((1,)), dma((LAST,)),
         ],
         compiler_params=pltpu.CompilerParams(
             collective_id=0, has_side_effects=True, vmem_limit_bytes=54 * 1024 * 1024
@@ -438,7 +524,7 @@
     ring, holders = lax.axis_size("ka"), lax.axis_size("occ")
     whole_square = pairs * holders == orbitals * orbitals
     fits = momenta == 2 and orbitals == 2 and holders == 2 and rounds == 2
-    even = ring % 2 == 0 and ring > 4 and auxiliary % LANES == 0
+    even = ring % 2 == 0 and ring > 6 and auxiliary % LANES == 0
     banded = virtuals % BAND == 0 and virtuals >= 2 * BAND
     chosen = fused if whole_square and fits and even and banded else general
     return chosen(factors, occupied_energy, virtual_energy, conserve, pair_lists)

time: 41.7 us -> 39.4 us (0.945)
  Pallas kernels: 40.8 us -> 38.5 us
    pallas_call x1, Pallas kernels: 40.8 us -> 38.5 us  [fused(): pl.pallas_call(functools.partial(fused_kernel, ring, virtuals, auxiliary)...]
where the time goes in v2:
time: 39.4 us; the launch traced here: 39.2 us
  Pallas kernels  38.5 us (98%)
  local copies, waits for them, and re-layouts  0.75 us (2%)
    pallas_call x1, Pallas kernels, fused(): pl.pallas_call(functools.partial(fused_kernel, ring, virtuals, auxiliary)...  38.5 us

profile of v2, /device:TPU:0, one launch (start us, length us, event | category | flops | bytes accessed | tf_op | source)
XLA Modules:
  0.0 39.2 jit_solution(16174022937355114524)
XLA Ops:
  0.0 38.5 %density.1 = f32[2,384,128]{2,1,0:T(8,128)S(1)} custom-call(s32[2,2]{1,0:T(2,128)} %conserve_hbm.1, f32[2]{0:T(128)} %occupied_hbm.1, bf16[2,192]{1,0:T(2,128)(2,1)} %energy_hbm.1, bf16[2,2,192,2,768]{4,3,2,1,0:T(2,128)(2,1)} %factors_ref.1), custom_call_target="tpu_custom_call" | custom-call | tf_op jit(solution)/shard_map/density/pallas_call | solution.py:481
  38.5 0.7 %copy.7 = f32[2,96,2,192]{3,2,1,0:T(2,128)} copy(f32[2,96,2,192]{3,2,1,0:T(2,128)S(1)} %bitcast.6) | data formatting | bytes 589824

commit v3 on v2

--- a/solution.py
+++ b/solution.py
@@ -11,7 +11,8 @@
 BAND = 64
 STEP = 16
 PIECE = 8
-LAST = 3
+LAST = 4
+MOST = 4
 
 
 def from_behind(array, axis, by):
@@ -97,9 +98,9 @@
 def fused_kernel(
     ring, virtuals, auxiliary,
     conserve_hbm, occupied_hbm, energy_hbm, factors_ref, out_ref,
-    conserve_ref, occupied_ref, energy_ref, own_raw, mate_raw, side, own, mate, energy_in, energy_left, inverse, products, total, outgoing, incoming,
+    conserve_ref, occupied_ref, energy_ref, own_raw, mate_raw, side, loan, own, mate, energy_in, energy_left, inverse, products, total, outgoing, incoming,
     small_sem, own_sem, far_send, far_recv, near_send, near_recv,
-    energy_send, energy_recv, swap_send, swap_recv, side_send, side_recv,
+    energy_send, energy_recv, swap_send, swap_recv, side_send, side_recv, loan_send, loan_recv,
 ):
     mesh_id = pl.DeviceIdType.MESH
     me = lax.axis_index("ka")
@@ -119,6 +120,14 @@
         return lax.rem(me + step + ring, ring)
 
     near = at(1 - 2 * odd)
+    lender = jnp.logical_and(lax.rem(me, 4) == 2, me != ring - 2)
+    carrier = jnp.logical_and(lax.rem(me, 4) == 0, me != ring - 4)
+
+    def lent(sender):
+        return jnp.minimum(2 + sender // 4, MOST)
+
+    def keeps(piece):
+        return jnp.logical_or(jnp.logical_not(lender), piece < pieces - lent(me))
 
     def own_copy(momentum, index):
         return pltpu.make_async_copy(
@@ -142,6 +151,14 @@
                 barrier, inc=1, device_id=(speaker, core), device_id_type=mesh_id
             )
 
+    @pl.when(carrier)
+    def _():
+        pl.semaphore_signal(barrier, inc=1, device_id=(at(2), core), device_id_type=mesh_id)
+
+    @pl.when(jnp.logical_and(lax.rem(me, 4) == 0, me != 0))
+    def _():
+        pl.semaphore_signal(barrier, inc=1, device_id=(at(-4), core), device_id_type=mesh_id)
+
     own_copy(core, 0).start()
     for copy in small_copies():
         copy.start()
@@ -190,6 +207,22 @@
             device_id=(0, core), device_id_type=mesh_id,
         )
 
+    def loan_copy(slot):
+        return pltpu.make_async_remote_copy(
+            src_ref=factors_ref.at[core, :, piece_rows(pieces - lent(me) + slot)],
+            dst_ref=loan.at[slot],
+            send_sem=far_send.at[0], recv_sem=loan_recv.at[slot],
+            device_id=(at(-2), core), device_id_type=mesh_id,
+        )
+
+    def loan_carry(slot):
+        piece = pieces - lent(me + 2) + slot
+        return pltpu.make_async_remote_copy(
+            src_ref=loan.at[slot], dst_ref=mate_raw.at[1, :, piece_rows(piece)],
+            send_sem=loan_send.at[slot], recv_sem=far_recv.at[piece],
+            device_id=(at(4), core), device_id_type=mesh_id,
+        )
+
     def energy_far():
         return pltpu.make_async_remote_copy(
             src_ref=energy_ref, dst_ref=energy_in.at[1],
@@ -204,7 +237,8 @@
             device_id=(near, core), device_id_type=mesh_id,
         )
 
-    greeters = jnp.where(jnp.logical_or(me == ring - 1, me == ring - 4), 4, 3)
+    extra = jnp.logical_or(jnp.logical_or(lender, carrier), me >= ring - 1)
+    greeters = jnp.where(jnp.logical_or(extra, me == ring - 4), 4, 3)
     pl.semaphore_wait(barrier, greeters)
 
     @pl.when(me == ring - 1)
@@ -212,8 +246,24 @@
         for slot in range(LAST):
             lend_copy(slot).start()
 
+    for slot in range(MOST):
+        @pl.when(jnp.logical_and(lender, slot < lent(me)))
+        def _():
+            loan_copy(slot).start()
+
+    late = me == ring - 6
+
+    def send_far(piece, carry):
+        @pl.when(keeps(piece))
+        def _():
+            far_copy(piece).start()
+
+        return carry
+
     def send_piece(piece, carry):
-        far_copy(piece).start()
+        @pl.when(jnp.logical_not(late))
+        def _():
+            send_far(piece, 0)
 
         @pl.when(odd == 0)
         def _():
@@ -328,7 +378,19 @@
     early = steps - (BAND // PIECE - 1)
     lax.fori_loop(0, early, shape_own, 0)
 
+    @pl.when(late)
+    def _():
+        lax.fori_loop(0, pieces, send_far, 0)
+
     def main_step(piece, carry):
+        @pl.when(jnp.logical_and(carrier, piece == jnp.where(me == 0, 6, pieces - 3)))
+        def _():
+            for slot in range(MOST):
+                @pl.when(slot < lent(me + 2))
+                def _():
+                    loan_copy(slot).wait_recv()
+                    loan_carry(slot).start()
+
         forward(piece)
 
         for slot in range(LAST):
@@ -337,9 +399,10 @@
                 lend_copy(slot).wait_recv()
                 carry_copy(slot).start()
 
-        @pl.when(jnp.logical_and(me == 0, piece == pieces - 3))
-        def _():
-            near_step(steps - 1)
+        for behind in (1, 2):
+            @pl.when(jnp.logical_and(me == 0, piece == pieces - 1 - 2 * behind))
+            def _():
+                near_step(steps - behind)
 
         @pl.when(piece == 1)
         def _():
@@ -423,16 +486,16 @@
         for momentum in range(2):
             out_ref[momentum] += jnp.where(chosen[second] == momentum, 0.0, incoming[second])
 
-    near_first = jnp.logical_or(me == 0, me == ring - 4)
+    near_first = jnp.logical_or(me == 0, jnp.logical_and(lax.rem(me, 4) == 0, me >= 8))
 
     @pl.when(near_first)
     def _():
         def near_rest():
             near_step(steps - 3)
-            near_step(steps - 2)
 
             @pl.when(me != 0)
             def _():
+                near_step(steps - 2)
                 near_step(steps - 1)
 
         def far_rest():
@@ -467,6 +530,11 @@
     @pl.when(jnp.logical_or(me == ring - 1, me == ring - 4))
     def _():
         sent(side, side_send.at[0])
+
+    for slot in range(MOST):
+        @pl.when(jnp.logical_and(carrier, slot < lent(me + 2)))
+        def _():
+            loan_carry(slot).wait_send()
 
 
 def fused(factors, occupied_energy, virtual_energy, conserve, pair_lists):
@@ -495,6 +563,7 @@
             pltpu.VMEM((momenta, orbitals, virtuals, parts, auxiliary), jnp.bfloat16),
             pltpu.VMEM((2, orbitals, virtuals, parts, auxiliary), jnp.bfloat16),
             pltpu.VMEM((LAST, orbitals, PIECE, parts, auxiliary), jnp.bfloat16),
+            pltpu.VMEM((MOST, orbitals, PIECE, parts, auxiliary), jnp.bfloat16),
             pltpu.VMEM((momenta, orbitals * virtuals, parts * auxiliary), jnp.bfloat16),
             pltpu.VMEM((2, bands, orbitals * 2 * BAND, parts * auxiliary), jnp.bfloat16),
             pltpu.VMEM((2, momenta, virtuals), jnp.bfloat16),
@@ -507,7 +576,7 @@
             dma((3,)), dma((2,)),
             dma((1,)), dma((pieces,)), dma((1,)), dma((virtuals // STEP,)),
             dma((2,)), dma((2,)), dma((2,)), dma((2,)),
-            dma((1,)), dma((LAST,)),
+            dma((1,)), dma((LAST,)), dma((MOST,)), dma((MOST,)),
         ],
         compiler_params=pltpu.CompilerParams(
             collective_id=0, has_side_effects=True, vmem_limit_bytes=54 * 1024 * 1024
@@ -524,7 +593,7 @@
     ring, holders = lax.axis_size("ka"), lax.axis_size("occ")
     whole_square = pairs * holders == orbitals * orbitals
     fits = momenta == 2 and orbitals == 2 and holders == 2 and rounds == 2
-    even = ring % 2 == 0 and ring > 6 and auxiliary % LANES == 0
+    even = ring % 4 == 0 and ring > 8 and auxiliary % LANES == 0
     banded = virtuals % BAND == 0 and virtuals >= 2 * BAND
     chosen = fused if whole_square and fits and even and banded else general
     return chosen(factors, occupied_energy, virtual_energy, conserve, pair_lists)

time: 39.4 us -> 38.6 us (0.980)
  Pallas kernels: 38.5 us -> 37.5 us
    pallas_call x1, Pallas kernels: 38.5 us -> 37.5 us  [fused(): pl.pallas_call(functools.partial(fused_kernel, ring, virtuals, auxiliary)...]
where the time goes in v3:
time: 38.6 us; the launch traced here: 38.2 us
  Pallas kernels  37.5 us (97%)
  local copies, waits for them, and re-layouts  0.75 us (2%)
    pallas_call x1, Pallas kernels, fused(): pl.pallas_call(functools.partial(fused_kernel, ring, virtuals, auxiliary)...  37.5 us

profile of v3, /device:TPU:0, one launch (start us, length us, event | category | flops | bytes accessed | tf_op | source)
XLA Modules:
  0.0 38.2 jit_solution(797804315470427605)
XLA Ops:
  0.0 37.5 %density.1 = f32[2,384,128]{2,1,0:T(8,128)S(1)} custom-call(s32[2,2]{1,0:T(2,128)} %conserve_hbm.1, f32[2]{0:T(128)} %occupied_hbm.1, bf16[2,192]{1,0:T(2,128)(2,1)} %energy_hbm.1, bf16[2,2,192,2,768]{4,3,2,1,0:T(2,128)(2,1)} %factors_ref.1), custom_call_target="tpu_custom_call" | custom-call | tf_op jit(solution)/shard_map/density/pallas_call | solution.py:549
  37.5 0.7 %copy.7 = f32[2,96,2,192]{3,2,1,0:T(2,128)} copy(f32[2,96,2,192]{3,2,1,0:T(2,128)S(1)} %bitcast.6) | data formatting | bytes 589824

commit v4 on v3

--- a/solution.py
+++ b/solution.py
@@ -12,7 +12,7 @@
 STEP = 16
 PIECE = 8
 LAST = 4
-MOST = 4
+MOST = 2
 
 
 def from_behind(array, axis, by):
@@ -98,9 +98,9 @@
 def fused_kernel(
     ring, virtuals, auxiliary,
     conserve_hbm, occupied_hbm, energy_hbm, factors_ref, out_ref,
-    conserve_ref, occupied_ref, energy_ref, own_raw, mate_raw, side, loan, own, mate, energy_in, energy_left, inverse, products, total, outgoing, incoming,
+    conserve_ref, occupied_ref, energy_ref, own_raw, mate_raw, side, own, mate, energy_in, energy_left, inverse, products, right_rows, total, outgoing, incoming, partial,
     small_sem, own_sem, far_send, far_recv, near_send, near_recv,
-    energy_send, energy_recv, swap_send, swap_recv, side_send, side_recv, loan_send, loan_recv,
+    energy_send, energy_recv, swap_send, swap_recv, side_send, side_recv,
 ):
     mesh_id = pl.DeviceIdType.MESH
     me = lax.axis_index("ka")
@@ -124,14 +124,17 @@
     carrier = jnp.logical_and(lax.rem(me, 4) == 0, me != ring - 4)
 
     def lent(sender):
-        return jnp.minimum(2 + sender // 4, MOST)
+        return jnp.where(sender == ring - 6, MOST, 2)
 
     def keeps(piece):
         return jnp.logical_or(jnp.logical_not(lender), piece < pieces - lent(me))
 
-    def own_copy(momentum, index):
+    def sent(done, semaphore):
+        pltpu.make_async_copy(done, done, semaphore).wait()
+
+    def own_copy(momentum):
         return pltpu.make_async_copy(
-            factors_ref.at[momentum], own_raw.at[momentum], own_sem.at[index]
+            factors_ref.at[momentum], own_raw.at[momentum], own_sem.at[0]
         )
 
     def small_copies():
@@ -159,10 +162,10 @@
     def _():
         pl.semaphore_signal(barrier, inc=1, device_id=(at(-4), core), device_id_type=mesh_id)
 
-    own_copy(core, 0).start()
+    own_copy(core).start()
     for copy in small_copies():
         copy.start()
-    own_copy(other, 1).start()
+    own_copy(other).start()
 
     def piece_rows(piece):
         return pl.ds(pl.multiple_of(piece * PIECE, PIECE), PIECE)
@@ -210,23 +213,23 @@
     def loan_copy(slot):
         return pltpu.make_async_remote_copy(
             src_ref=factors_ref.at[core, :, piece_rows(pieces - lent(me) + slot)],
-            dst_ref=loan.at[slot],
-            send_sem=far_send.at[0], recv_sem=loan_recv.at[slot],
+            dst_ref=side.at[slot],
+            send_sem=far_send.at[0], recv_sem=side_recv.at[slot],
             device_id=(at(-2), core), device_id_type=mesh_id,
         )
 
     def loan_carry(slot):
         piece = pieces - lent(me + 2) + slot
         return pltpu.make_async_remote_copy(
-            src_ref=loan.at[slot], dst_ref=mate_raw.at[1, :, piece_rows(piece)],
-            send_sem=loan_send.at[slot], recv_sem=far_recv.at[piece],
+            src_ref=side.at[slot], dst_ref=mate_raw.at[1, :, piece_rows(piece)],
+            send_sem=side_send.at[0], recv_sem=far_recv.at[piece],
             device_id=(at(4), core), device_id_type=mesh_id,
         )
 
     def energy_far():
         return pltpu.make_async_remote_copy(
             src_ref=energy_ref, dst_ref=energy_in.at[1],
-            send_sem=energy_send.at[1], recv_sem=energy_recv.at[1],
+            send_sem=energy_send.at[0], recv_sem=energy_recv.at[1],
             device_id=(at(2), core), device_id_type=mesh_id,
         )
 
@@ -287,8 +290,7 @@
         mirror = lax.rem(2 - lax.rem(conserve_ref[0, slot], 2), 2)
         chosen.append(jnp.where(mirror == core, 0, 1))
 
-    own_copy(core, 0).wait()
-    own_copy(other, 1).wait()
+    sent(own_raw, own_sem.at[0])
 
     def forward(piece):
         far_copy(piece).wait_recv()
@@ -301,17 +303,15 @@
         for momentum in range(2):
             for orbital in range(2):
                 row = pl.ds(pl.multiple_of(orbital * virtuals + step * STEP, STEP), STEP)
-                for part in range(2):
-                    own[momentum, row, pl.ds(part * auxiliary, auxiliary)] = own_raw[
-                        momentum, orbital, step_rows(step), part, :
-                    ]
+                raw = own_raw[momentum, orbital, step_rows(step)]
+                own[momentum, row, :] = raw.reshape(STEP, 2 * auxiliary)
         return carry
 
     def shape_mate(slot, step):
         band = step // per_band
         for orbital in range(2):
-            real = mate_raw[slot, orbital, step_rows(step), 0, :]
-            imaginary = mate_raw[slot, orbital, step_rows(step), 1, :]
+            both = mate_raw[slot, orbital, step_rows(step)].reshape(STEP, 2 * auxiliary)
+            real, imaginary = both[:, :auxiliary], both[:, auxiliary:]
             first = orbital * 2 * BAND + lax.rem(step, per_band) * STEP
             plain = pl.ds(pl.multiple_of(first, STEP), STEP)
             turned = pl.ds(pl.multiple_of(first + BAND, STEP), STEP)
@@ -344,31 +344,49 @@
 
     sign = jnp.where(lax.broadcasted_iota(jnp.int32, (virtuals, LANES), 1) < BAND, -1.0, 1.0)
 
-    def add_band(slot, band):
+    def amplitude_of(slot, band, i, j, start, rows):
+        value = products[slot, pl.ds(i * virtuals + start, rows), j * LANES : (j + 1) * LANES]
+        return value * inverse[slot, band, i + j, pl.ds(start, rows), :]
+
+    def band_products(slot, band):
         momentum = jnp.where(slot == 1, chosen[1], chosen[0])
-        products[...] = lax.dot_general(
+        products[slot] = lax.dot_general(
             own[momentum], mate[slot, band], (((1,), (1,)), ((), ())),
             preferred_element_type=jnp.float32,
         )
-        amplitudes = {}
+
+    def band_right(slot, band):
+        rounded, turned = [], []
         for i in range(2):
             for j in range(2):
-                value = products[i * virtuals : (i + 1) * virtuals, j * LANES : (j + 1) * LANES]
-                amplitudes[i, j] = value * inverse[slot, band, i + j]
-        combined, rounded, turned = [], [], []
+                this = amplitude_of(slot, band, i, j, 0, virtuals)
+                rounded.append(this.astype(jnp.bfloat16))
+                turned.append((pltpu.roll(this, BAND, 1) * sign).astype(jnp.bfloat16))
+        kinds = [jnp.concatenate(kind, axis=1) for kind in (rounded, turned)]
+        blocks = [
+            kind[start : start + LANES] for start in range(0, virtuals, LANES) for kind in kinds
+        ]
+        return jnp.concatenate(blocks, axis=0)
+
+    def band_left(slot, band, start, rows):
+        this = {}
         for i in range(2):
             for j in range(2):
-                this = amplitudes[i, j]
-                combined.append((2.0 * this - amplitudes[j, i]).astype(jnp.bfloat16))
-                rounded.append(this.astype(jnp.bfloat16))
-                turned.append((pltpu.roll(this, BAND, 1) * sign).astype(jnp.bfloat16))
-        left = jnp.concatenate(combined, axis=1)
-        spare = jnp.zeros((tiles * LANES - virtuals, left.shape[1]), jnp.bfloat16)
-        for part, pieces_of in enumerate((rounded, turned)):
-            right = jnp.concatenate([jnp.concatenate(pieces_of, axis=1), spare], axis=0)
-            total[slot, part] += lax.dot_general(
-                left, right, (((1,), (1,)), ((), ())), preferred_element_type=jnp.float32
-            )
+                this[i, j] = amplitude_of(slot, band, i, j, start, rows)
+        combined = [
+            (2.0 * this[i, j] - this[j, i]).astype(jnp.bfloat16) for i in range(2) for j in range(2)
+        ]
+        return jnp.concatenate(combined, axis=1)
+
+    def times(left, right):
+        return lax.dot_general(
+            left, right, (((1,), (1,)), ((), ())), preferred_element_type=jnp.float32
+        )
+
+    def add_band(slot, band):
+        band_products(slot, band)
+        left = band_left(slot, band, 0, virtuals)
+        total[slot] += times(left, band_right(slot, band))
 
     def near_step(step):
         near_arrival(step).wait()
@@ -377,10 +395,6 @@
     total[...] = jnp.zeros_like(total)
     early = steps - (BAND // PIECE - 1)
     lax.fori_loop(0, early, shape_own, 0)
-
-    @pl.when(late)
-    def _():
-        lax.fori_loop(0, pieces, send_far, 0)
 
     def main_step(piece, carry):
         @pl.when(jnp.logical_and(carrier, piece == jnp.where(me == 0, 6, pieces - 3)))
@@ -393,6 +407,10 @@
 
         forward(piece)
 
+        @pl.when(jnp.logical_and(late, piece == 1))
+        def _():
+            lax.fori_loop(0, pieces, send_far, 0)
+
         for slot in range(LAST):
             @pl.when(jnp.logical_and(me == ring - 4, piece == slot + 8))
             def _():
@@ -400,7 +418,7 @@
                 carry_copy(slot).start()
 
         for behind in (1, 2):
-            @pl.when(jnp.logical_and(me == 0, piece == pieces - 1 - 2 * behind))
+            @pl.when(jnp.logical_and(me == 0, piece == pieces - 5 - 2 * behind))
             def _():
                 near_step(steps - behind)
 
@@ -418,9 +436,11 @@
         def _():
             shape_mate(1, piece // per_step)
 
-        @pl.when(jnp.logical_and(even_piece, piece >= 4))
-        def _():
-            near_step(piece // 2 - 2)
+        lag = 4
+
+        @pl.when(jnp.logical_and(even_piece, piece >= lag))
+        def _():
+            near_step((piece - lag) // 2)
 
         @pl.when(piece < steps - early)
         def _():
@@ -444,66 +464,98 @@
     def swap_copy(slot):
         return pltpu.make_async_remote_copy(
             src_ref=outgoing.at[slot], dst_ref=incoming.at[slot],
-            send_sem=swap_send.at[slot], recv_sem=swap_recv.at[slot],
+            send_sem=swap_send.at[0], recv_sem=swap_recv.at[slot],
             device_id=(me, other), device_id_type=mesh_id,
         )
 
     def half_rows(which):
         return pl.ds(pl.multiple_of(which * half, half), half)
 
-    def places():
-        for part in range(2):
-            for tile in range(tiles):
-                yield part, pl.ds(tile * LANES, LANES), pl.ds(tile * 2 + part, half, stride)
-
-    def swap_start(slot):
-        for part, lanes, spots in places():
-            outgoing[slot, spots, :] = total[slot, part, half_rows(other), lanes]
+    def spots(part, tile):
+        return pl.ds(tile * 2 + part, half, stride)
+
+    def rows_of(slot, which):
+        start = pl.multiple_of(which * half, half)
+        left = band_left(slot, bands - 1, start, half)
+        return total[slot, pl.ds(start, half), :] + times(left, right_rows[slot])
+
+    def own_half(slot, keep):
+        known = rows_of(slot, core)
+        for momentum in range(2):
+            mine = jnp.where(chosen[slot] == momentum, known, 0.0)
+            partial[momentum] = partial[momentum] + mine if keep else mine
+
+    def send_half(slot, apart):
+        def multiply():
+            band_products(slot, bands - 1)
+            right_rows[slot] = band_right(slot, bands - 1)
+            outgoing[slot] = rows_of(slot, other)
+
+        if apart:
+            pl.when(core >= 0)(multiply)
+        else:
+            multiply()
         swap_copy(slot).start()
 
-    def sent(done, semaphore):
-        pltpu.make_async_copy(done, done, semaphore).wait()
-
-    def finish(first, second, before_first, before_second):
+    def close_band(slot, keep, later):
+        send_half(slot, len(later) > 0)
+
+        @pl.when(core >= 0)
+        def _():
+            own_half(slot, keep)
+            for behind in later:
+                own_half(behind, True)
+
+    def store_out(momentum, value):
+        for tile in range(tiles):
+            first = value[:, 2 * tile * LANES : (2 * tile + 1) * LANES]
+            out_ref[momentum, spots(0, tile), :] = first
+            if (tile + 1) * LANES <= virtuals:
+                second = value[:, (2 * tile + 1) * LANES : (2 * tile + 2) * LANES]
+            else:
+                second = pltpu.roll(first, LANES // 2, 1)
+            out_ref[momentum, spots(1, tile), :] = second
+
+    def finish(first, second, before_first, before_second, together):
+        def theirs(slot, momentum):
+            return jnp.where(chosen[slot] == momentum, 0.0, incoming[slot])
+
         before_first()
-        add_band(first, bands - 1)
-        swap_start(first)
+        if together:
+            send_half(first, True)
+        else:
+            close_band(first, False, ())
+        before_second()
+        close_band(second, not together, (first,) if together else ())
+        sent(own_raw.at[core], far_send.at[0])
+        swap_copy(first).wait_recv()
         for momentum in range(2):
-            for part, lanes, spots in places():
-                known = total[first, part, half_rows(core), lanes]
-                out_ref[momentum, spots, :] = jnp.where(chosen[first] == momentum, known, 0.0)
-        before_second()
-        add_band(second, bands - 1)
-        swap_start(second)
-        swap_copy(first).wait()
+            partial[momentum] += theirs(first, momentum)
+        swap_copy(second).wait_recv()
         for momentum in range(2):
-            out_ref[momentum] += jnp.where(chosen[first] == momentum, 0.0, incoming[first])
-            for part, lanes, spots in places():
-                known = total[second, part, half_rows(core), lanes]
-                out_ref[momentum, spots, :] += jnp.where(chosen[second] == momentum, known, 0.0)
-        sent(own_raw.at[core], far_send.at[0])
-        swap_copy(second).wait()
-        for momentum in range(2):
-            out_ref[momentum] += jnp.where(chosen[second] == momentum, 0.0, incoming[second])
-
-    near_first = jnp.logical_or(me == 0, jnp.logical_and(lax.rem(me, 4) == 0, me >= 8))
+            store_out(momentum, partial[momentum] + theirs(second, momentum))
+
+    near_first = me == 0
 
     @pl.when(near_first)
     def _():
-        def near_rest():
-            near_step(steps - 3)
-
-            @pl.when(me != 0)
-            def _():
-                near_step(steps - 2)
-                near_step(steps - 1)
-
         def far_rest():
             for piece in range(pieces - per_step, pieces):
                 forward(piece)
             shape_mate(1, steps - 1)
 
-        finish(0, 1, near_rest, far_rest)
+        def near_rest():
+            @pl.when(me == 0)
+            def _():
+                near_step(steps - 3)
+
+            @pl.when(me != 0)
+            def _():
+                near_step(steps - 2)
+                far_rest()
+                near_step(steps - 1)
+
+        finish(0, 1, near_rest, lambda: pl.when(me == 0)(far_rest), True)
 
     @pl.when(jnp.logical_not(near_first))
     def _():
@@ -514,10 +566,10 @@
             shape_mate(1, steps - 1)
             near_step(steps - 2)
 
-        finish(1, 0, far_rest, lambda: near_step(steps - 1))
-
-    energy_far().wait_send()
-    energy_near(False).wait_send()
+        finish(1, 0, far_rest, lambda: near_step(steps - 1), False)
+
+    sent(energy_in, energy_send.at[0])
+    sent(outgoing, swap_send.at[0])
 
     @pl.when(me == 1)
     def _():
@@ -531,10 +583,10 @@
     def _():
         sent(side, side_send.at[0])
 
-    for slot in range(MOST):
-        @pl.when(jnp.logical_and(carrier, slot < lent(me + 2)))
-        def _():
-            loan_carry(slot).wait_send()
+    for count in (MOST,):
+        @pl.when(jnp.logical_and(carrier, lent(me + 2) == count))
+        def _():
+            sent(side.at[pl.ds(0, count)], side_send.at[0])
 
 
 def fused(factors, occupied_energy, virtual_energy, conserve, pair_lists):
@@ -563,20 +615,21 @@
             pltpu.VMEM((momenta, orbitals, virtuals, parts, auxiliary), jnp.bfloat16),
             pltpu.VMEM((2, orbitals, virtuals, parts, auxiliary), jnp.bfloat16),
             pltpu.VMEM((LAST, orbitals, PIECE, parts, auxiliary), jnp.bfloat16),
-            pltpu.VMEM((MOST, orbitals, PIECE, parts, auxiliary), jnp.bfloat16),
             pltpu.VMEM((momenta, orbitals * virtuals, parts * auxiliary), jnp.bfloat16),
             pltpu.VMEM((2, bands, orbitals * 2 * BAND, parts * auxiliary), jnp.bfloat16),
             pltpu.VMEM((2, momenta, virtuals), jnp.bfloat16),
             pltpu.VMEM((momenta, virtuals, LANES), jnp.float32),
             pltpu.VMEM((2, bands, 3, virtuals, LANES), jnp.float32),
-            pltpu.VMEM((orbitals * virtuals, orbitals * 2 * BAND), jnp.float32),
-            pltpu.VMEM((2, 2, virtuals, tiles * LANES), jnp.float32),
-            pltpu.VMEM((2, *packed), jnp.float32),
-            pltpu.VMEM((2, *packed), jnp.float32),
-            dma((3,)), dma((2,)),
+            pltpu.VMEM((2, orbitals * virtuals, orbitals * 2 * BAND), jnp.float32),
+            pltpu.VMEM((2, 2 * virtuals, orbitals * orbitals * LANES), jnp.bfloat16),
+            pltpu.VMEM((2, virtuals, 2 * virtuals), jnp.float32),
+            pltpu.VMEM((2, half, 2 * virtuals), jnp.float32),
+            pltpu.VMEM((2, half, 2 * virtuals), jnp.float32),
+            pltpu.VMEM((2, half, 2 * virtuals), jnp.float32),
+            dma((3,)), dma((1,)),
             dma((1,)), dma((pieces,)), dma((1,)), dma((virtuals // STEP,)),
-            dma((2,)), dma((2,)), dma((2,)), dma((2,)),
-            dma((1,)), dma((LAST,)), dma((MOST,)), dma((MOST,)),
+            dma((1,)), dma((2,)), dma((1,)), dma((2,)),
+            dma((1,)), dma((LAST,)),
         ],
         compiler_params=pltpu.CompilerParams(
             collective_id=0, has_side_effects=True, vmem_limit_bytes=54 * 1024 * 1024

time: 38.6 us -> 37.3 us (0.966)
  Pallas kernels: 37.5 us -> 36.4 us
    pallas_call x1, Pallas kernels: 37.5 us -> 36.4 us  [fused(): pl.pallas_call(functools.partial(fused_kernel, ring, virtuals, auxiliary)...]
where the time goes in v4:
time: 37.3 us; the launch traced here: 37.1 us
  Pallas kernels  36.4 us (98%)
  local copies, waits for them, and re-layouts  0.75 us (2%)
    pallas_call x1, Pallas kernels, fused(): pl.pallas_call(functools.partial(fused_kernel, ring, virtuals, auxiliary)...  36.4 us
    unnamed x1, local copies, waits for them, and re-layouts  0.75 us

profile of v4, /device:TPU:0, one launch (start us, length us, event | category | flops | bytes accessed | tf_op | source)
XLA Modules:
  0.0 37.1 jit_solution(4477612284420290459)
XLA Ops:
  0.0 36.4 %density.1 = f32[2,384,128]{2,1,0:T(8,128)S(1)} custom-call(s32[2,2]{1,0:T(2,128)} %conserve_hbm.1, f32[2]{0:T(128)} %occupied_hbm.1, bf16[2,192]{1,0:T(2,128)(2,1)} %energy_hbm.1, bf16[2,2,192,2,768]{4,3,2,1,0:T(2,128)(2,1)} %factors_ref.1), custom_call_target="tpu_custom_call" | custom-call | tf_op jit(solution)/shard_map/density/pallas_call | solution.py:601
  36.4 0.7 %copy.7 = f32[2,96,2,192]{3,2,1,0:T(2,128)} copy(f32[2,96,2,192]{3,2,1,0:T(2,128)S(1)} %bitcast.6) | data formatting | bytes 589824
